TPU v7x, 32 devices: a whole 2x2x4 slice. The times are simulated.
32 devices in a mesh: grp: 2 (over y), seq: 16 (over z, x, core).
Axes of the slice: x: 2, y: 2, z: 4, core: 2. Of those that a mesh axis runs over, the one named last changes fastest.
Arguments:
- hidden: bfloat16 [16, 4096], P('grp'), parts along dimension 0, may hold values from -6 to 6
- mix_gain: float32 [4096], replicated, may hold values from 0.5 to 1.5
- in_gate_input: bfloat16 [4096, 2048], P(None, 'seq'), may hold values from -0.09375 to 0.09375
- in_step: bfloat16 [4096, 16], P(None, 'seq'), may hold values from -0.09375 to 0.09375
- in_groups: bfloat16 [4096, 2048], P(None, 'seq'), may hold values from -0.09375 to 0.09375
- conv_input: bfloat16 [16, 3, 1024], P('grp', None, 'seq'), parts along dimension 0, may hold values from -6 to 6
- conv_groups: bfloat16 [16, 3, 2048], P('grp', None, 'seq'), parts along dimension 0, may hold values from -6 to 6
- taps_input: float32 [5, 1024], P(None, 'seq'), may hold values from -0.6 to 0.6
- taps_groups: float32 [5, 2048], P(None, 'seq'), may hold values from -0.6 to 0.6
- decay_rate: float32 [16], P('seq'), may hold values from 1 to 16
- step_bias: float32 [16], P('seq'), may hold values from -4 to -1
- skip_gain: float32 [16], P('seq'), may hold values from 0.1 to 1.9
- norm_gain: float32 [1024], P('seq'), may hold values from 0.5 to 1.5
- out_mixer: bfloat16 [1024, 4096], P('seq'), may hold values from -0.1875 to 0.1875
- ssm_state: float32 [16, 16, 64, 128], P('grp', 'seq'), parts along dimension 0, may hold values from -6 to 6
- attn_gain: float32 [4096], P('seq'), may hold values from 0.5 to 1.5
- w_qkv: bfloat16 [4096, 6144], P('seq'), may hold values from -0.09375 to 0.09375
- w_out: bfloat16 [4096, 4096], P(None, 'seq'), may hold values from -0.09375 to 0.09375
- kv_cache: bfloat16 [64, 128, 2048], P(('grp', 'seq')), parts along dimension 0, may hold values from -310 to 310
- page_table: int32 [16, 4], P('grp'), parts along dimension 0, may hold values from 0 to 31, as said below
- lengths: int32 [16], P('grp'), parts along dimension 0, may hold values from 1 to 512
Outputs:
- final: bfloat16 [16, 4096], P('grp', 'seq'), parts along dimension 0
- new_state: float32 [16, 16, 64, 128], P('grp', 'seq'), parts along dimension 0
- new_kv: bfloat16 [16, 2048], P('grp'), parts along dimension 0
There are 2 independent parts, one for each index of `grp`. A program takes and returns all parts, laid end to end along the dimension named above; an argument that names none is the same for every part. Nothing has to cross between parts.
Inputs may be any that keep to these rules, and one draw needn't show every extreme that they name: `page_table`: each number 0 to 31 appears exactly once.
All inputs are finite; a program needn't handle non-finite values.
Results may differ from a plain program's by a relative error of at most 0.018.
Values may be sent and summed in bfloat16 or wider, within the bound.
No kernel may reach another device: no remote copies, remote signals or barrier semaphores. Data moves between devices by JAX's collectives and lax.ppermute only.
A program may use at most 64 MiB of HBM per device.

v0:
```python
import jax
import jax.numpy as jnp
from jax import lax
from jax.sharding import PartitionSpec as P

QH = 32
KVH = 8
HD = 128
STATE = 128
GROUPS = 8
epsilon = 1e-05
lowest = -1e30


def merged(array, axis, combine):
    everything = jax.tree.map(
        lambda part, kind: lax.all_gather(part.astype(kind), axis),
        array,
        (jnp.bfloat16, jnp.bfloat16, jnp.bfloat16),
    )

    def take(k):
        return jax.tree.map(lambda part, own: part[k].astype(own.dtype), everything, array)

    return lax.fori_loop(
        1, lax.axis_size(axis), lambda k, so_far: combine(so_far, take(k)), take(0)
    )


def conv_step(state, fresh, taps):
    window = jnp.concatenate([state.astype(jnp.float32), fresh[:, None, :]], axis=1)
    summed = jnp.sum(window * taps[:-1][None], axis=1) + taps[-1][None]
    return jax.nn.silu(summed)


def merge_pair(first, second):
    peak = jnp.maximum(first[0], second[0])
    first_factor = jnp.exp(first[0] - peak)
    second_factor = jnp.exp(second[0] - peak)
    total = first[1] * first_factor + second[1] * second_factor
    values = first[2] * first_factor[..., None] + second[2] * second_factor[..., None]
    return (peak, total, values)


def finish(peak_prior, total_prior, values_prior, query_rows, key_rows, value_rows, scale):
    own = jnp.sum(query_rows.astype(jnp.float32) * key_rows.astype(jnp.float32), axis=-1) * scale
    peak = jnp.maximum(peak_prior, own)
    old_factor = jnp.exp(peak_prior - peak)
    own_weight = jnp.exp(own - peak)
    summed = values_prior * old_factor[..., None] + own_weight[..., None] * value_rows.astype(
        jnp.float32
    )
    return (summed / (total_prior * old_factor + own_weight)[..., None]).astype(jnp.bfloat16)


def shards(
    hidden,
    mix_gain,
    in_gate_input,
    in_step,
    in_groups,
    conv_input,
    conv_groups,
    taps_input,
    taps_groups,
    decay_rate,
    step_bias,
    skip_gain,
    norm_gain,
    out_mixer,
    ssm_state,
    attn_gain,
    w_qkv,
    w_out,
    kv_cache,
    page_table,
    lengths,
):
    highest = lax.Precision.HIGHEST
    count_seq = lax.axis_size("seq")
    position = lax.axis_index("seq")
    requests = hidden.shape[0]
    width = hidden.shape[1]
    heads_here = in_step.shape[1]
    head_width = in_gate_input.shape[1] // (2 * heads_here)
    heads_total = heads_here * count_seq
    per_group = heads_total // GROUPS
    stream = hidden.astype(jnp.float32)
    normed = (
        stream * lax.rsqrt(jnp.mean(stream * stream, axis=-1, keepdims=True) + epsilon) * mix_gain
    ).astype(jnp.bfloat16)
    gate_input = jnp.dot(normed, in_gate_input, preferred_element_type=jnp.float32).reshape(
        requests, heads_here, 2, head_width
    )
    gate_part = gate_input[:, :, 0]
    input_part = gate_input[:, :, 1].reshape(requests, heads_here * head_width)
    step_raw = jnp.dot(normed, in_step, preferred_element_type=jnp.float32)
    group_raw = jnp.dot(normed, in_groups, preferred_element_type=jnp.float32)
    conv_out = conv_step(conv_input, input_part, taps_input).reshape(
        requests, heads_here, head_width
    )
    group_conv = conv_step(conv_groups, group_raw, taps_groups).astype(jnp.bfloat16)
    group_all = lax.all_gather(group_conv, "seq", axis=1, tiled=True).astype(jnp.float32)
    inject = group_all[:, : GROUPS * STATE].reshape(requests, GROUPS, STATE)
    readout = group_all[:, GROUPS * STATE :].reshape(requests, GROUPS, STATE)
    head_ids = position * heads_here + jnp.arange(heads_here, dtype=jnp.int32)
    select = (head_ids[:, None] % GROUPS == jnp.arange(GROUPS, dtype=jnp.int32)[None, :]).astype(
        jnp.float32
    )
    inject_heads = jnp.einsum("hg,rgn->rhn", select, inject, precision=highest)
    readout_heads = jnp.einsum("hg,rgn->rhn", select, readout, precision=highest)
    step_size = jax.nn.softplus(step_raw + step_bias)
    decay = jnp.exp(-decay_rate * step_size)
    new_state = (
        decay[:, :, None, None] * ssm_state
        + (step_size[:, :, None] * conv_out)[:, :, :, None] * inject_heads[:, :, None, :]
    )
    ssm_out = (
        jnp.einsum("rhpn,rhn->rhp", new_state, readout_heads, precision=highest)
        + skip_gain[None, :, None] * conv_out
    )
    gated = ssm_out * jax.nn.silu(gate_part)
    head_squares = jnp.sum(gated * gated, axis=-1)
    all_squares = lax.all_gather(head_squares, "seq", axis=1, tiled=True)
    group_means = jnp.sum(all_squares.reshape(requests, per_group, GROUPS), axis=1) / (
        per_group * head_width
    )
    own_means = jnp.einsum("hg,rg->rh", select, group_means, precision=highest)
    normed_mix = (
        gated
        * lax.rsqrt(own_means + epsilon)[..., None]
        * norm_gain.reshape(heads_here, head_width)
    ).astype(jnp.bfloat16)
    mixer_term = jnp.dot(
        normed_mix.reshape(requests, heads_here * head_width),
        out_mixer,
        preferred_element_type=jnp.float32,
    )
    mixer = lax.psum_scatter(mixer_term, "seq", scatter_dimension=1, tiled=True)
    columns = width // count_seq
    stream_cols = lax.dynamic_slice_in_dim(stream, position * columns, columns, 1)
    middle = (stream_cols + mixer).astype(jnp.bfloat16)
    middle_f = middle.astype(jnp.float32)
    scaled = (middle_f * attn_gain).astype(jnp.bfloat16)
    partial_proj = jnp.dot(scaled, w_qkv, preferred_element_type=jnp.float32)
    partial_sq = jnp.sum(middle_f * middle_f, axis=-1)
    projected, total_sq = lax.psum((partial_proj, partial_sq), "seq")
    qkv = (projected * lax.rsqrt(total_sq / width + epsilon)[:, None]).astype(jnp.bfloat16)
    group_size = QH // KVH
    queries = qkv[:, : QH * HD]
    fresh_keys = qkv[:, QH * HD : (QH + KVH) * HD].reshape(requests, KVH, HD)
    fresh_values = qkv[:, (QH + KVH) * HD :].reshape(requests, KVH, HD)
    new_kv = qkv[:, QH * HD :]
    scale = 1.0 / HD**0.5
    pages_here = kv_cache.shape[0]
    page_len = kv_cache.shape[1]
    pages_req = page_table.shape[1]
    slots = position * pages_here + jnp.arange(pages_here, dtype=jnp.int32)
    matches = page_table[None, :, :] == slots[:, None, None]
    owner_hit = jnp.any(matches, axis=2)
    owner = owner_hit.astype(jnp.bfloat16)
    logical = jnp.sum(
        jnp.any(matches, axis=1) * jnp.arange(pages_req, dtype=jnp.int32)[None, :], axis=1
    )
    page_length = jnp.sum(jnp.where(owner_hit, lengths[None, :], 0), axis=1)
    token_pos = logical[:, None] * page_len + jnp.arange(page_len, dtype=jnp.int32)[None, :]
    live = token_pos < page_length[:, None]
    page_queries = jnp.dot(owner, queries, preferred_element_type=jnp.float32).astype(jnp.bfloat16)
    page_queries = page_queries.reshape(pages_here, KVH, group_size, HD)
    cached = kv_cache.reshape(pages_here, page_len, 2, KVH, HD)
    scores = (
        jnp.einsum(
            "pgjd,ptgd->pgjt", page_queries, cached[:, :, 0], preferred_element_type=jnp.float32
        )
        * scale
    )
    live_mask = live[:, None, None, :]
    masked = jnp.where(live_mask, scores, lowest)
    page_peak = jnp.max(masked, axis=-1)
    weights = jnp.where(live_mask, jnp.exp(masked - page_peak[..., None]), 0.0)
    page_total = jnp.sum(weights, axis=-1)
    page_values = jnp.einsum(
        "pgjt,ptgd->pgjd",
        weights.astype(jnp.bfloat16),
        cached[:, :, 1],
        preferred_element_type=jnp.float32,
    )
    owner_mask = owner_hit[:, :, None, None]
    request_peak = jnp.max(jnp.where(owner_mask, page_peak[:, None], lowest), axis=0)
    factor = jnp.where(owner_mask, jnp.exp(page_peak[:, None] - request_peak[None]), 0.0)
    request_total = jnp.einsum("prgj,pgj->rgj", factor, page_total, precision=highest)
    request_values = jnp.einsum("prgj,pgjd->rgjd", factor, page_values, precision=highest)
    request_peak = request_peak.reshape(requests, QH)
    request_total = request_total.reshape(requests, QH)
    request_values = request_values.reshape(requests, QH, HD)
    query_rows = queries.reshape(requests, QH, HD)
    key_rows = jnp.repeat(fresh_keys, group_size, axis=1)
    value_rows = jnp.repeat(fresh_values, group_size, axis=1)
    peak_all, total_all, values_all = merged(
        (request_peak, request_total, request_values), "seq", merge_pair
    )
    attended = finish(
        peak_all, total_all, values_all, query_rows, key_rows, value_rows, scale
    ).reshape(requests, QH * HD)
    final = (middle_f + jnp.dot(attended, w_out, preferred_element_type=jnp.float32)).astype(
        jnp.bfloat16
    )
    return (final, new_state, new_kv)


def solution(mesh):
    placed = (
        P("grp", None),
        P(),
        P(None, "seq"),
        P(None, "seq"),
        P(None, "seq"),
        P("grp", None, "seq"),
        P("grp", None, "seq"),
        P(None, "seq"),
        P(None, "seq"),
        P("seq"),
        P("seq"),
        P("seq"),
        P("seq"),
        P("seq", None),
        P("grp", "seq", None, None),
        P("seq"),
        P("seq", None),
        P(None, "seq"),
        P(("grp", "seq"), None, None),
        P("grp", None),
        P("grp"),
    )
    return jax.shard_map(
        shards,
        mesh=mesh,
        in_specs=placed,
        out_specs=(P("grp", "seq"), P("grp", "seq", None, None), P("grp", None)),
        check_vma=False,
    )
```

profile of v0, /device:TPU:0, one launch (start us, length us, event | category | flops | bytes accessed | tf_op | source)
XLA Modules:
  0.0 282.0 jit_solution(5698425340825484725)
XLA Ops:
  12.0 1.6 convolution_bitcast_fusion.1
  13.6 23.2 %all_gather.18 = bf16[8,2048]{1,0:T(8,128)(2,1)S(1)} all-gather(bf16[8,128]{1,0:T(8,128)(2,1)S(1)} %multiply_convert_fusion.3), channel_id=1, replica_groups=mesh['grp'=2,'seq'=16] {'seq'}, dimensions={1}, use_global_device_ids=true | all-gather | bytes 34816 | tf_op jit(solution)/shard_map/all_gather | solution.py:103
  36.8 1.6 fusion.68
  41.4 1.1 multiply_exponential_fusion
  42.5 1.1 multiply_add_fusion
  44.3 17.4 %all-gather = f32[16,1,8]{2,1,0:T(1,128)S(1)} all-gather(f32[1,1,8]{2,1,0:T(1,128)S(1)} %bitcast.157), channel_id=1, replica_groups=mesh['grp'=2,'seq'=16] {'seq'}, dimensions={0}, use_global_device_ids=true | all-gather | bytes 544 | tf_op jit(solution)/shard_map/all_gather | solution.py:124
  62.0 1.9 fusion.46
  65.1 2.3 copy.80
  67.5 50.7 %reduce-scatter.2.cloned.1.call-done = f32[8,256]{1,0:T(8,128)} async-done(((f32[8,4096]{1,0:T(8,128)}), f32[8,256]{1,0:T(8,128)}) %reduce-scatter.2.cloned.1.call-update) | async-done | bytes 8208 | tf_op jit(solution)/shard_map/reduce_scatter | solution.py:139
  119.0 1.2 fusion.42
  120.3 29.5 %psum.15 = f32[8]{0:T(128)S(1)} all-reduce(f32[8]{0:T(128)S(1)} %get-tuple-element.214), channel_id=1, replica_groups=mesh['grp'=2,'seq'=16] {'seq'}, use_global_device_ids=true, to_apply=%region_12.13 | all-reduce | flops 8 | bytes 64 | tf_op jit(solution)/shard_map/psum | solution.py:147
  149.8 61.6 %all-reduce.2.cloned.1.call-done = f32[8,6144]{1,0:T(8,128)} async-done(((f32[8,6144]{1,0:T(8,128)}), f32[8,6144]{1,0:T(8,128)}) %all-reduce.2.cloned.1.call-update) | async-done | bytes 196624 | tf_op jit(solution)/shard_map/psum | solution.py:147
  211.4 1.0 multiply_convert_fusion
  212.6 1.4 fusion.73
  214.1 1.5 fusion.8
  218.7 19.5 %all_gather.21 = bf16[16,8,32]{2,1,0:T(8,128)(2,1)S(1)} all-gather(bf16[1,8,32]{2,1,0:T(8,128)(2,1)S(1)} %copy.84), channel_id=1, replica_groups=mesh['grp'=2,'seq'=16] {'seq'}, dimensions={0}, use_global_device_ids=true | all-gather | bytes 8704 | tf_op jit(solution)/shard_map/all_gather | solution.py:17
  238.2 17.8 %all_gather.20 = bf16[16,8,32]{2,1,0:T(8,128)(2,1)S(1)} all-gather(bf16[1,8,32]{2,1,0:T(8,128)(2,1)S(1)} %copy.83), channel_id=1, replica_groups=mesh['grp'=2,'seq'=16] {'seq'}, dimensions={0}, use_global_device_ids=true | all-gather | bytes 8704 | tf_op jit(solution)/shard_map/all_gather | solution.py:17
  256.9 15.8 %while.19 = (s32[]{:T(128)}, f32[8,32]{1,0:T(8,128)S(1)}, f32[8,32]{1,0:T(8,128)S(1)}, f32[8,32,128]{2,1,0:T(8,128)S(1)}, bf16[16,8,32]{2,1,0:T(8,128)(2,1)S(1)}...) while((s32[]{:T(128)}, f32[8,32]{1,0:T(8,128)S(1)}, ...), condition=%wide.region_17.18_spmd, body=%wide.region_16.17_spmd.sunk | while | flops 133125 | bytes 337047 | solution.py:25
  256.9 1.0 fusion.87
  258.0 1.0 fusion.87
  263.2 1.0 fusion.87
  267.4 1.0 fusion.87
  268.5 1.0 fusion.87
  272.9 2.6 fusion.4
  (103 shorter events, 23.8 us)
Async XLA Ops:
  7.2 111.9 %copy-start = (bf16[256,6144]{1,0:T(8,128)(2,1)S(1)}, bf16[256,6144]{1,0:T(8,128)(2,1)}, u32[]{:S(2)}) copy-start(bf16[256,6144]{1,0:T(8,128)(2,1)} %param.39) | copy-start | bytes 9437188
  7.2 56.9 %copy-start.1 = (bf16[8,4096]{1,0:T(8,128)(2,1)S(1)}, bf16[8,4096]{1,0:T(8,128)(2,1)}, u32[]{:S(2)}) copy-start(bf16[8,4096]{1,0:T(8,128)(2,1)} %param.23) | copy-start | bytes 196612
  7.2 54.9 %copy-start.5 = (f32[64]{0:T(128)S(1)}, f32[64]{0:T(128)}, u32[]{:S(2)}) copy-start(f32[64]{0:T(128)} %param.35) | copy-start | bytes 772
  7.2 57.5 %copy-start.3 = (s32[8,4]{0,1:T(4,128)S(1)}, s32[8,4]{0,1:T(4,128)}, u32[]{:S(2)}) copy-start(s32[8,4]{0,1:T(4,128)} %param.42) | copy-start | bytes 388
  7.2 111.0 %reduce-scatter.2.cloned.1.call-start = ((), (), s32[]{:S(2)}) async-start(), calls=%async_computation.1 | async-start | bytes 139264 | tf_op jit(solution)/shard_map/reduce_scatter | solution.py:139
  12.0 55.4 %copy-start.6 = (s32[8]{0:T(128)S(1)}, s32[8]{0:T(128)}, u32[]{:S(2)}) copy-start(s32[8]{0:T(128)} %param.43) | copy-start | bytes 100
  12.0 107.1 %copy-start.4 = (f32[256]{0:T(256)S(1)}, f32[256]{0:T(256)}, u32[]{:S(2)}) copy-start(f32[256]{0:T(256)} %param.38) | copy-start | bytes 3076
  43.6 76.6 %copy-start.2 = (f32[8,1,64,128]{3,2,1,0:T(8,128)}, f32[8,1,64,128]{3,2,1,0:T(8,128)S(1)}, u32[]{:S(2)}) copy-start(f32[8,1,64,128]{3,2,1,0:T(8,128)S(1)} %multiply_add_fusion) | copy-start | bytes 786436
  64.0 147.4 %all-reduce.2.cloned.1.call-start = ((), (), s32[]{:S(2)}) async-start(), calls=%async_computation.2 | async-start | bytes 393216 | tf_op jit(solution)/shard_map/psum | solution.py:147
  120.3 135.7 %all-gather.3.cloned.1.call-start = ((), (), s32[]{:S(2)}) async-start(), calls=%async_computation.3 | async-start | bytes 1114112 | tf_op jit(solution)/shard_map/all_gather | solution.py:17
Sparse Core Ops, SparseCore 0:
  64.1 54.0 reduce-scatter.1
  121.6 89.7 all-reduce.1
  217.1 36.9 all-gather.2
where the time goes:
time: 284 us; the launch traced here: 282 us
  waiting for transfers between devices  112 us (39%)
  blocking collectives  107 us (38%)
  other arithmetic  23.6 us (8%)
  between operations  15.9 us (6%)
  matrix products  14.8 us (5%)
  local copies, waits for them, and re-layouts  7.37 us (3%)
    psum x1, waiting for transfers between devices, shards(): projected, total_sq = lax.psum((partial_proj, partial_sq), 'seq')  61.6 us
    reduce_scatter x1, waiting for transfers between devices, shards(): mixer = lax.psum_scatter(mixer_term, 'seq', scatter_dimension=1, tiled=True)  50.7 us
    all_gather x2, blocking collectives, merged(): lax.all_gather(part.astype(kind), axis)  37.3 us
    psum x1, blocking collectives, shards(): projected, total_sq = lax.psum((partial_proj, partial_sq), 'seq')  29.5 us
    all_gather x1, blocking collectives, shards(): lax.all_gather(group_conv, 'seq', axis=1, tiled=True).astype(jnp.float32)  23.2 us
    all_gather x1, blocking collectives, shards(): all_squares = lax.all_gather(head_squares, 'seq', axis=1, tiled=True)  17.4 us
    add x15, other arithmetic, merge_pair(): first[2] * first_factor[..., None] + second[2] * second_factor[..., None]  15 us
  transfers between devices with their start and end apart: 3, of which 2 were waited for; matrix products, arithmetic and copies ran while one was open for 2% of the time, Pallas kernels for 0%

commit v1 on v0

--- a/solution.py
+++ b/solution.py
@@ -1,7 +1,9 @@
+import functools
 import jax
 import jax.numpy as jnp
 from jax import lax
 from jax.sharding import PartitionSpec as P
+from jax.lax import axis_index, axis_size, ppermute
 
 QH = 32
 KVH = 8
@@ -10,6 +12,21 @@
 GROUPS = 8
 epsilon = 1e-05
 lowest = -1e30
+
+
+def clear_field(inp, d0):
+    n_slots = axis_size("seq")
+    main = sorted(((b, (b + 1) % n_slots) for b in range(n_slots)))
+    left_arr = inp
+    sheets = [left_arr]
+    for ix in [*range(1, n_slots)]:
+        left_arr = ppermute(left_arr, "seq", main)
+        sheets.insert(0, left_arr)
+    inter = jnp.concatenate(sheets, d0)
+    return jnp.roll(inter, (axis_index("seq") + 1) * inp.shape[d0], d0)
+
+
+kinds_lead = functools.partial(clear_field, d0=1)
 
 
 def merged(array, axis, combine):
@@ -121,7 +138,7 @@
     )
     gated = ssm_out * jax.nn.silu(gate_part)
     head_squares = jnp.sum(gated * gated, axis=-1)
-    all_squares = lax.all_gather(head_squares, "seq", axis=1, tiled=True)
+    all_squares = kinds_lead(head_squares)
     group_means = jnp.sum(all_squares.reshape(requests, per_group, GROUPS), axis=1) / (
         per_group * head_width
     )

time: 284 us -> 351 us (1.24)
  waiting for transfers between devices: 112 us -> 195 us
  blocking collectives: 107 us -> 90 us
    ppermute x0 -> x15, waiting for transfers between devices: none -> 80.4 us  [clear_field(): left_arr = ppermute(left_arr, 'seq', main)]
    all_gather x1 -> x0, blocking collectives: 17.4 us -> none  [shards(): all_squares = lax.all_gather(head_squares, 'seq', axis=1, tiled=True)]
  transfers between devices with their start and end apart: 3 -> 18, of which waited for: 2 -> 17; matrix products, arithmetic and copies ran while one was open for 2% -> 2% of each run, Pallas kernels for 0% -> 0%
where the time goes in v1:
time: 351 us; the launch traced here: 349 us
  waiting for transfers between devices  195 us (56%)
  blocking collectives  90 us (26%)
  other arithmetic  23.6 us (7%)
  between operations  16 us (5%)
  matrix products  14.8 us (4%)
  local copies, waits for them, and re-layouts  8.78 us (3%)
    ppermute x15, waiting for transfers between devices, clear_field(): left_arr = ppermute(left_arr, 'seq', main)  80.4 us
    psum x1, waiting for transfers between devices, shards(): projected, total_sq = lax.psum((partial_proj, partial_sq), 'seq')  61.6 us
    reduce_scatter x1, waiting for transfers between devices, shards(): mixer = lax.psum_scatter(mixer_term, 'seq', scatter_dimension=1, tiled=True)  52.9 us
    all_gather x2, blocking collectives, merged(): lax.all_gather(part.astype(kind), axis)  37.3 us
    psum x1, blocking collectives, shards(): projected, total_sq = lax.psum((partial_proj, partial_sq), 'seq')  29.5 us
    all_gather x1, blocking collectives, shards(): lax.all_gather(group_conv, 'seq', axis=1, tiled=True).astype(jnp.float32)  23.2 us
    add x15, other arithmetic, merge_pair(): first[2] * first_factor[..., None] + second[2] * second_factor[..., None]  15 us
  transfers between devices with their start and end apart: 18, of which 17 were waited for; matrix products, arithmetic and copies ran while one was open for 2% of the time, Pallas kernels for 0%

profile of v1, /device:TPU:0, one launch (start us, length us, event | category | flops | bytes accessed | tf_op | source)
XLA Modules:
  0.0 349.0 jit_solution(11654629354982226430)
XLA Ops:
  13.6 23.2 %all_gather.15 = bf16[8,2048]{1,0:T(8,128)(2,1)S(1)} all-gather(bf16[8,128]{1,0:T(8,128)(2,1)S(1)} %multiply_convert_fusion.3), channel_id=1, replica_groups=mesh['grp'=2,'seq'=16] {'seq'}, dimensions={1}, use_global_device_ids=true | all-gather | bytes 34816 | tf_op jit(solution)/shard_map/all_gather | solution.py:120
  45.8 2.3 copy.173
  50.1 5.6 %collective-permute-done.1 = f32[8,1]{0,1:T(1,128)S(1)} collective-permute-done((f32[8,1]{0,1:T(1,128)S(1)}, f32[8,1]{0,1:T(1,128)S(1)}, u32[]{:S(2)}, u32[]{:S(2)}) %collective-permute-start.1) | collective-permute-done | bytes 64 | tf_op jit(solution)/shard_map/ppermute | solution.py:23
  55.8 5.6 %collective-permute-done.2 = f32[8,1]{0,1:T(1,128)S(1)} collective-permute-done((f32[8,1]{0,1:T(1,128)S(1)}, f32[8,1]{0,1:T(1,128)S(1)}, u32[]{:S(2)}, u32[]{:S(2)}) %collective-permute-start.2) | collective-permute-done | bytes 64 | tf_op jit(solution)/shard_map/ppermute | solution.py:23
  61.5 5.6 %collective-permute-done.3 = f32[8,1]{0,1:T(1,128)S(1)} collective-permute-done((f32[8,1]{0,1:T(1,128)S(1)}, f32[8,1]{0,1:T(1,128)S(1)}, u32[]{:S(2)}, u32[]{:S(2)}) %collective-permute-start.3) | collective-permute-done | bytes 64 | tf_op jit(solution)/shard_map/ppermute | solution.py:23
  67.2 5.6 %collective-permute-done.4 = f32[8,1]{0,1:T(1,128)S(1)} collective-permute-done((f32[8,1]{0,1:T(1,128)S(1)}, f32[8,1]{0,1:T(1,128)S(1)}, u32[]{:S(2)}, u32[]{:S(2)}) %collective-permute-start.4) | collective-permute-done | bytes 64 | tf_op jit(solution)/shard_map/ppermute | solution.py:23
  72.9 5.6 %collective-permute-done.5 = f32[8,1]{0,1:T(1,128)S(1)} collective-permute-done((f32[8,1]{0,1:T(1,128)S(1)}, f32[8,1]{0,1:T(1,128)S(1)}, u32[]{:S(2)}, u32[]{:S(2)}) %collective-permute-start.5) | collective-permute-done | bytes 64 | tf_op jit(solution)/shard_map/ppermute | solution.py:23
  78.6 5.6 %collective-permute-done.6 = f32[8,1]{0,1:T(1,128)S(1)} collective-permute-done((f32[8,1]{0,1:T(1,128)S(1)}, f32[8,1]{0,1:T(1,128)S(1)}, u32[]{:S(2)}, u32[]{:S(2)}) %collective-permute-start.6) | collective-permute-done | bytes 64 | tf_op jit(solution)/shard_map/ppermute | solution.py:23
  84.3 5.6 %collective-permute-done.7 = f32[8,1]{0,1:T(1,128)S(1)} collective-permute-done((f32[8,1]{0,1:T(1,128)S(1)}, f32[8,1]{0,1:T(1,128)S(1)}, u32[]{:S(2)}, u32[]{:S(2)}) %collective-permute-start.7) | collective-permute-done | bytes 64 | tf_op jit(solution)/shard_map/ppermute | solution.py:23
  90.0 5.6 %collective-permute-done.8 = f32[8,1]{0,1:T(1,128)S(1)} collective-permute-done((f32[8,1]{0,1:T(1,128)S(1)}, f32[8,1]{0,1:T(1,128)S(1)}, u32[]{:S(2)}, u32[]{:S(2)}) %collective-permute-start.8) | collective-permute-done | bytes 64 | tf_op jit(solution)/shard_map/ppermute | solution.py:23
  95.6 5.6 %collective-permute-done.9 = f32[8,1]{0,1:T(1,128)S(1)} collective-permute-done((f32[8,1]{0,1:T(1,128)S(1)}, f32[8,1]{0,1:T(1,128)S(1)}, u32[]{:S(2)}, u32[]{:S(2)}) %collective-permute-start.9) | collective-permute-done | bytes 64 | tf_op jit(solution)/shard_map/ppermute | solution.py:23
  101.3 5.6 %collective-permute-done.10 = f32[8,1]{0,1:T(1,128)S(1)} collective-permute-done((f32[8,1]{0,1:T(1,128)S(1)}, f32[8,1]{0,1:T(1,128)S(1)}, u32[]{:S(2)}, u32[]{:S(2)}) %collective-permute-start.10) | collective-permute-done | bytes 64 | tf_op jit(solution)/shard_map/ppermute | solution.py:23
  107.0 5.6 %collective-permute-done.11 = f32[8,1]{0,1:T(1,128)S(1)} collective-permute-done((f32[8,1]{0,1:T(1,128)S(1)}, f32[8,1]{0,1:T(1,128)S(1)}, u32[]{:S(2)}, u32[]{:S(2)}) %collective-permute-start.11) | collective-permute-done | bytes 64 | tf_op jit(solution)/shard_map/ppermute | solution.py:23
  112.7 5.6 %collective-permute-done.12 = f32[8,1]{0,1:T(1,128)S(1)} collective-permute-done((f32[8,1]{0,1:T(1,128)S(1)}, f32[8,1]{0,1:T(1,128)S(1)}, u32[]{:S(2)}, u32[]{:S(2)}) %collective-permute-start.12) | collective-permute-done | bytes 64 | tf_op jit(solution)/shard_map/ppermute | solution.py:23
  118.4 5.6 %collective-permute-done.13 = f32[8,1]{0,1:T(1,128)S(1)} collective-permute-done((f32[8,1]{0,1:T(1,128)S(1)}, f32[8,1]{0,1:T(1,128)S(1)}, u32[]{:S(2)}, u32[]{:S(2)}) %collective-permute-start.13) | collective-permute-done | bytes 64 | tf_op jit(solution)/shard_map/ppermute | solution.py:23
  124.1 5.6 %collective-permute-done.14 = f32[8,1]{0,1:T(1,128)S(1)} collective-permute-done((f32[8,1]{0,1:T(1,128)S(1)}, f32[8,1]{0,1:T(1,128)S(1)}, u32[]{:S(2)}, u32[]{:S(2)}) %collective-permute-start.14) | collective-permute-done | bytes 64 | tf_op jit(solution)/shard_map/ppermute | solution.py:23
  130.2 2.0 fusion.46
  132.3 52.9 %reduce-scatter.2.cloned.1.call-done = f32[8,256]{1,0:T(8,128)} async-done(((f32[8,4096]{1,0:T(8,128)}), f32[8,256]{1,0:T(8,128)}) %reduce-scatter.2.cloned.1.call-update) | async-done | bytes 8208 | tf_op jit(solution)/shard_map/reduce_scatter | solution.py:156
  187.3 29.5 %psum.15 = f32[8]{0:T(128)S(1)} all-reduce(f32[8]{0:T(128)S(1)} %get-tuple-element.214), channel_id=1, replica_groups=mesh['grp'=2,'seq'=16] {'seq'}, use_global_device_ids=true, to_apply=%region_12.13 | all-reduce | flops 8 | bytes 64 | tf_op jit(solution)/shard_map/psum | solution.py:164
  216.9 61.6 %all-reduce.2.cloned.1.call-done = f32[8,6144]{1,0:T(8,128)} async-done(((f32[8,6144]{1,0:T(8,128)}), f32[8,6144]{1,0:T(8,128)}) %all-reduce.2.cloned.1.call-update) | async-done | bytes 196624 | tf_op jit(solution)/shard_map/psum | solution.py:164
  285.8 19.5 %all_gather.17 = bf16[16,8,32]{2,1,0:T(8,128)(2,1)S(1)} all-gather(bf16[1,8,32]{2,1,0:T(8,128)(2,1)S(1)} %copy.177), channel_id=1, replica_groups=mesh['grp'=2,'seq'=16] {'seq'}, dimensions={0}, use_global_device_ids=true | all-gather | bytes 8704 | tf_op jit(solution)/shard_map/all_gather | solution.py:34
  305.3 17.8 %all_gather.16 = bf16[16,8,32]{2,1,0:T(8,128)(2,1)S(1)} all-gather(bf16[1,8,32]{2,1,0:T(8,128)(2,1)S(1)} %copy.176), channel_id=1, replica_groups=mesh['grp'=2,'seq'=16] {'seq'}, dimensions={0}, use_global_device_ids=true | all-gather | bytes 8704 | tf_op jit(solution)/shard_map/all_gather | solution.py:34
  323.9 15.8 %while.19 = (s32[]{:T(128)}, f32[8,32]{1,0:T(8,128)S(1)}, f32[8,32]{1,0:T(8,128)S(1)}, f32[8,32,128]{2,1,0:T(8,128)S(1)}, bf16[16,8,32]{2,1,0:T(8,128)(2,1)S(1)}...) while((s32[]{:T(128)}, f32[8,32]{1,0:T(8,128)S(1)}, ...), condition=%wide.region_17.18_spmd, body=%wide.region_16.17_spmd.sunk | while | flops 133125 | bytes 337047 | solution.py:42
  339.9 2.6 fusion.4
  (149 shorter events, 42.8 us)
Async XLA Ops:
  7.2 178.9 %copy-start = (bf16[256,6144]{1,0:T(8,128)(2,1)S(1)}, bf16[256,6144]{1,0:T(8,128)(2,1)}, u32[]{:S(2)}) copy-start(bf16[256,6144]{1,0:T(8,128)(2,1)} %param.39) | copy-start | bytes 9437188
  7.2 38.2 %copy-start.3 = (s32[8,4]{0,1:T(4,128)S(1)}, s32[8,4]{0,1:T(4,128)}, u32[]{:S(2)}) copy-start(s32[8,4]{0,1:T(4,128)} %param.42) | copy-start | bytes 388
  7.2 40.9 %copy-start.6 = (s32[8]{0:T(128)S(1)}, s32[8]{0:T(128)}, u32[]{:S(2)}) copy-start(s32[8]{0:T(128)} %param.43) | copy-start | bytes 100
  7.2 123.0 %copy-start.5 = (f32[64]{0:T(128)S(1)}, f32[64]{0:T(128)}, u32[]{:S(2)}) copy-start(f32[64]{0:T(128)} %param.35) | copy-start | bytes 772
  7.2 178.0 %reduce-scatter.2.cloned.1.call-start = ((), (), s32[]{:S(2)}) async-start(), calls=%async_computation.1 | async-start | bytes 139264 | tf_op jit(solution)/shard_map/reduce_scatter | solution.py:156
  13.5 172.5 %copy-start.4 = (f32[256]{0:T(256)S(1)}, f32[256]{0:T(256)}, u32[]{:S(2)}) copy-start(f32[256]{0:T(256)} %param.38) | copy-start | bytes 3076
  43.6 143.7 %copy-start.2 = (f32[8,1,64,128]{3,2,1,0:T(8,128)}, f32[8,1,64,128]{3,2,1,0:T(8,128)S(1)}, u32[]{:S(2)}) copy-start(f32[8,1,64,128]{3,2,1,0:T(8,128)S(1)} %multiply_add_fusion) | copy-start | bytes 786436
  44.3 5.7 %collective-permute-start = (f32[8,1]{0,1:T(1,128)S(1)}, f32[8,1]{0,1:T(1,128)S(1)}, u32[]{:S(2)}, u32[]{:S(2)}) collective-permute-start(f32[8,1]{0,1:T(1,128)S(1)} %bitcast.153), channel_id=1, source_target_pairs={{0,1},{1,2},{2,3},{3,4},{4,5},{5,6},{6,7},{7,8},{8,9},{9,10},{10,1... | collective-permute-start | bytes 104 | tf_op jit(solution)/shard_map/ppermute | solution.py:23
  50.0 5.7 %collective-permute-start.1 = (f32[8,1]{0,1:T(1,128)S(1)}, f32[8,1]{0,1:T(1,128)S(1)}, u32[]{:S(2)}, u32[]{:S(2)}) collective-permute-start(f32[8,1]{0,1:T(1,128)S(1)} %collective-permute-done), channel_id=1, source_target_pairs={{0,1},{1,2},{2,3},{3,4},{4,5},{5,6},{6,7},{7,8},{8,9},{9,10},{10,1... | collective-permute-start | bytes 104 | tf_op jit(solution)/shard_map/ppermute | solution.py:23
  55.7 5.7 %collective-permute-start.2 = (f32[8,1]{0,1:T(1,128)S(1)}, f32[8,1]{0,1:T(1,128)S(1)}, u32[]{:S(2)}, u32[]{:S(2)}) collective-permute-start(f32[8,1]{0,1:T(1,128)S(1)} %collective-permute-done.1), channel_id=1, source_target_pairs={{0,1},{1,2},{2,3},{3,4},{4,5},{5,6},{6,7},{7,8},{8,9},{9,10},{10,1... | collective-permute-start | bytes 104 | tf_op jit(solution)/shard_map/ppermute | solution.py:23
  61.4 5.7 %collective-permute-start.3 = (f32[8,1]{0,1:T(1,128)S(1)}, f32[8,1]{0,1:T(1,128)S(1)}, u32[]{:S(2)}, u32[]{:S(2)}) collective-permute-start(f32[8,1]{0,1:T(1,128)S(1)} %collective-permute-done.2), channel_id=1, source_target_pairs={{0,1},{1,2},{2,3},{3,4},{4,5},{5,6},{6,7},{7,8},{8,9},{9,10},{10,1... | collective-permute-start | bytes 104 | tf_op jit(solution)/shard_map/ppermute | solution.py:23
  67.1 5.7 %collective-permute-start.4 = (f32[8,1]{0,1:T(1,128)S(1)}, f32[8,1]{0,1:T(1,128)S(1)}, u32[]{:S(2)}, u32[]{:S(2)}) collective-permute-start(f32[8,1]{0,1:T(1,128)S(1)} %collective-permute-done.3), channel_id=1, source_target_pairs={{0,1},{1,2},{2,3},{3,4},{4,5},{5,6},{6,7},{7,8},{8,9},{9,10},{10,1... | collective-permute-start | bytes 104 | tf_op jit(solution)/shard_map/ppermute | solution.py:23
  72.8 5.7 %collective-permute-start.5 = (f32[8,1]{0,1:T(1,128)S(1)}, f32[8,1]{0,1:T(1,128)S(1)}, u32[]{:S(2)}, u32[]{:S(2)}) collective-permute-start(f32[8,1]{0,1:T(1,128)S(1)} %collective-permute-done.4), channel_id=1, source_target_pairs={{0,1},{1,2},{2,3},{3,4},{4,5},{5,6},{6,7},{7,8},{8,9},{9,10},{10,1... | collective-permute-start | bytes 104 | tf_op jit(solution)/shard_map/ppermute | solution.py:23
  78.5 5.7 %collective-permute-start.6 = (f32[8,1]{0,1:T(1,128)S(1)}, f32[8,1]{0,1:T(1,128)S(1)}, u32[]{:S(2)}, u32[]{:S(2)}) collective-permute-start(f32[8,1]{0,1:T(1,128)S(1)} %collective-permute-done.5), channel_id=1, source_target_pairs={{0,1},{1,2},{2,3},{3,4},{4,5},{5,6},{6,7},{7,8},{8,9},{9,10},{10,1... | collective-permute-start | bytes 104 | tf_op jit(solution)/shard_map/ppermute | solution.py:23
  84.2 5.7 %collective-permute-start.7 = (f32[8,1]{0,1:T(1,128)S(1)}, f32[8,1]{0,1:T(1,128)S(1)}, u32[]{:S(2)}, u32[]{:S(2)}) collective-permute-start(f32[8,1]{0,1:T(1,128)S(1)} %collective-permute-done.6), channel_id=1, source_target_pairs={{0,1},{1,2},{2,3},{3,4},{4,5},{5,6},{6,7},{7,8},{8,9},{9,10},{10,1... | collective-permute-start | bytes 104 | tf_op jit(solution)/shard_map/ppermute | solution.py:23
  89.9 5.7 %collective-permute-start.8 = (f32[8,1]{0,1:T(1,128)S(1)}, f32[8,1]{0,1:T(1,128)S(1)}, u32[]{:S(2)}, u32[]{:S(2)}) collective-permute-start(f32[8,1]{0,1:T(1,128)S(1)} %collective-permute-done.7), channel_id=1, source_target_pairs={{0,1},{1,2},{2,3},{3,4},{4,5},{5,6},{6,7},{7,8},{8,9},{9,10},{10,1... | collective-permute-start | bytes 104 | tf_op jit(solution)/shard_map/ppermute | solution.py:23
  95.6 5.7 %collective-permute-start.9 = (f32[8,1]{0,1:T(1,128)S(1)}, f32[8,1]{0,1:T(1,128)S(1)}, u32[]{:S(2)}, u32[]{:S(2)}) collective-permute-start(f32[8,1]{0,1:T(1,128)S(1)} %collective-permute-done.8), channel_id=1, source_target_pairs={{0,1},{1,2},{2,3},{3,4},{4,5},{5,6},{6,7},{7,8},{8,9},{9,10},{10,1... | collective-permute-start | bytes 104 | tf_op jit(solution)/shard_map/ppermute | solution.py:23
  101.3 5.7 %collective-permute-start.10 = (f32[8,1]{0,1:T(1,128)S(1)}, f32[8,1]{0,1:T(1,128)S(1)}, u32[]{:S(2)}, u32[]{:S(2)}) collective-permute-start(f32[8,1]{0,1:T(1,128)S(1)} %collective-permute-done.9), channel_id=1, source_target_pairs={{0,1},{1,2},{2,3},{3,4},{4,5},{5,6},{6,7},{7,8},{8,9},{9,10},{10,1... | collective-permute-start | bytes 104 | tf_op jit(solution)/shard_map/ppermute | solution.py:23
  106.9 5.7 %collective-permute-start.11 = (f32[8,1]{0,1:T(1,128)S(1)}, f32[8,1]{0,1:T(1,128)S(1)}, u32[]{:S(2)}, u32[]{:S(2)}) collective-permute-start(f32[8,1]{0,1:T(1,128)S(1)} %collective-permute-done.10), channel_id=1, source_target_pairs={{0,1},{1,2},{2,3},{3,4},{4,5},{5,6},{6,7},{7,8},{8,9},{9,10},{10,1... | collective-permute-start | bytes 104 | tf_op jit(solution)/shard_map/ppermute | solution.py:23
  112.6 5.7 %collective-permute-start.12 = (f32[8,1]{0,1:T(1,128)S(1)}, f32[8,1]{0,1:T(1,128)S(1)}, u32[]{:S(2)}, u32[]{:S(2)}) collective-permute-start(f32[8,1]{0,1:T(1,128)S(1)} %collective-permute-done.11), channel_id=1, source_target_pairs={{0,1},{1,2},{2,3},{3,4},{4,5},{5,6},{6,7},{7,8},{8,9},{9,10},{10,1... | collective-permute-start | bytes 104 | tf_op jit(solution)/shard_map/ppermute | solution.py:23
  118.3 5.7 %collective-permute-start.13 = (f32[8,1]{0,1:T(1,128)S(1)}, f32[8,1]{0,1:T(1,128)S(1)}, u32[]{:S(2)}, u32[]{:S(2)}) collective-permute-start(f32[8,1]{0,1:T(1,128)S(1)} %collective-permute-done.12), channel_id=1, source_target_pairs={{0,1},{1,2},{2,3},{3,4},{4,5},{5,6},{6,7},{7,8},{8,9},{9,10},{10,1... | collective-permute-start | bytes 104 | tf_op jit(solution)/shard_map/ppermute | solution.py:23
  124.0 5.7 %collective-permute-start.14 = (f32[8,1]{0,1:T(1,128)S(1)}, f32[8,1]{0,1:T(1,128)S(1)}, u32[]{:S(2)}, u32[]{:S(2)}) collective-permute-start(f32[8,1]{0,1:T(1,128)S(1)} %collective-permute-done.13), channel_id=1, source_target_pairs={{0,1},{1,2},{2,3},{3,4},{4,5},{5,6},{6,7},{7,8},{8,9},{9,10},{10,1... | collective-permute-start | bytes 104 | tf_op jit(solution)/shard_map/ppermute | solution.py:23
  132.2 146.3 %all-reduce.2.cloned.1.call-start = ((), (), s32[]{:S(2)}) async-start(), calls=%async_computation.2 | async-start | bytes 393216 | tf_op jit(solution)/shard_map/psum | solution.py:164
  187.3 135.7 %all-gather.2.cloned.1.call-start = ((), (), s32[]{:S(2)}) async-start(), calls=%async_computation.3 | async-start | bytes 1114112 | tf_op jit(solution)/shard_map/all_gather | solution.py:34
  (1 other events, 37.6 us)
Sparse Core Ops, SparseCore 0:
  132.3 52.8 reduce-scatter.1
  188.7 89.7 all-reduce.1
  284.1 36.9 all-gather.1
